TPU v7x, 32 devices: a whole 2x2x4 slice. The times are simulated.
32 devices in a mesh: groups: 2 (over x), rows: 16 (over z, y, core).
Axes of the slice: x: 2, y: 2, z: 4, core: 2. Of those that a mesh axis runs over, the one named last changes fastest.
Arguments:
- frames: bfloat16 [16384, 2560], P(('groups', 'rows')), parts along dimension 0, may hold values from -6 to 6
- offsets: int32 [4096], P(('groups', 'rows')), parts along dimension 0, may hold values from 0 to 8173, as said below
- neighbours: int32 [32, 4096], P(None, ('groups', 'rows')), parts along dimension 1, may hold values from 0 to 2047, as said below
- initial_codes: int32 [32, 4096], P(None, ('groups', 'rows')), parts along dimension 1, may hold values from -1048576 to 1048575
- embed_weight: bfloat16 [2560, 256], replicated, may hold values from -0.125 to 0.125
- embed_bias: float32 [256], replicated, may hold values from -0.9 to 0.9
Outputs:
- affinity: float32 [32, 4096], P(None, ('groups', 'rows')), parts along dimension 1
- vectors: float32 [32, 4096], P(None, ('groups', 'rows')), parts along dimension 1
There are 2 independent parts, one for each index of `groups`. A program takes and returns all parts, laid end to end along the dimension named above; an argument that names none is the same for every part. Nothing has to cross between parts.
Inputs may be any that keep to these rules, and one draw needn't show every extreme that they name: `offsets`: the window of row i starts in the block of 512 frames numbered i // 128 and its 19 frames end before frame 8192. `neighbours`: the 32 columns of row i are distinct and differ from i; the k-th is (i + d) mod 2048 with 1 + k s <= d <= (k + 1) s, where s = 63.
All inputs are finite; a program needn't handle non-finite values.
Results may differ from a plain program's by a relative error of at most 0.012.
The roundings to bfloat16 on the way count: a program that leaves them out, or rounds other values in their place, can miss the bound.
Values may be sent and summed in bfloat16 or wider, within the bound.
No kernel may reach another device: no remote copies, remote signals or barrier semaphores. Data moves between devices by JAX's collectives and lax.ppermute only.
A program may use at most 64 MiB of HBM per device.

v0:
```python
import jax
import jax.numpy as jnp
from jax import lax
from jax.sharding import PartitionSpec as P

WIN = 19
ITERS = 3
epsilon = 1e-06
sharpness = 8.0
seed_scale = 2.0 ** (-20)


def from_behind(block, axis, distance):
    devices = range(lax.axis_size(axis))
    route = [(i - distance, i) for i in devices if i - distance in devices]
    return lax.ppermute(block, axis, route)


def block_width(length, shard_rows):
    shards = length // shard_rows
    chosen = 1
    for factor in range(1, shards + 1):
        if shards % factor == 0 and factor * shard_rows <= 4096:
            chosen = factor
    return chosen * shard_rows


def on_device(frames, offsets, neighbours, initial_codes, embed_weight, embed_bias):
    own_rows = offsets.shape[0]
    own_frames = frames.shape[0]
    kept = neighbours.shape[0]
    my_index = lax.axis_index("rows")
    next_frames = from_behind(frames[: WIN - 1], "rows", -1)
    extended = jnp.concatenate([frames, next_frames], axis=0)
    window_start = offsets - my_index * own_frames
    positions = jnp.arange(extended.shape[0], dtype=jnp.int32)[None, :]
    begins = window_start[:, None]
    window_mask = ((positions >= begins) & (positions < begins + WIN)).astype(jnp.bfloat16)
    window_sums = jnp.dot(window_mask, extended, preferred_element_type=jnp.float32)
    pooled = (window_sums * (1.0 / WIN)).astype(jnp.bfloat16)
    embedded = jnp.dot(pooled, embed_weight, preferred_element_type=jnp.float32) + embed_bias
    squares = jnp.sum(embedded * embedded, axis=1, keepdims=True)
    unit_rows = (embedded * lax.rsqrt(squares + epsilon)).astype(jnp.bfloat16)
    portion = lax.all_gather(unit_rows, "rows", axis=0, tiled=True)
    length = portion.shape[0]
    block_cols = block_width(length, own_rows)

    def one_block(block_index, carried):
        first_col = block_index * block_cols
        candidates = lax.dynamic_slice_in_dim(portion, first_col, block_cols, 0)
        scores = lax.dot_general(
            unit_rows, candidates, (((1,), (1,)), ((), ())), preferred_element_type=jnp.float32
        )
        relative = neighbours - first_col
        inside = (relative >= 0) & (relative < block_cols)
        picked = jnp.take_along_axis(scores, jnp.clip(relative, 0, block_cols - 1).T, axis=1).T
        return carried + jnp.where(inside, picked, 0.0)

    cosine = lax.fori_loop(
        0, length // block_cols, one_block, jnp.zeros((kept, own_rows), jnp.float32)
    )
    affinity = jnp.exp(sharpness * (cosine - 1.0))
    vectors = initial_codes.astype(jnp.float32) * seed_scale
    vec_count = vectors.shape[0]
    carried = vectors
    for turn_index in range(ITERS):
        gathered = lax.all_gather(carried, "rows", axis=1, tiled=True)
        if turn_index > 0:
            gram_matrix = jnp.dot(gathered, gathered.T, precision=lax.Precision.HIGHEST)
            cholesky_factor = jnp.linalg.cholesky(gram_matrix)
            gathered = jax.scipy.linalg.solve_triangular(cholesky_factor, gathered, lower=True)
        current = lax.dynamic_slice_in_dim(gathered, my_index * own_rows, own_rows, 1)
        forward = jnp.sum(affinity[None] * jnp.take(gathered, neighbours, axis=1), axis=1)
        spread = (
            jnp.zeros((vec_count, gathered.shape[1]), jnp.float32)
            .at[:, neighbours.reshape(-1)]
            .add((affinity[None] * current[:, None, :]).reshape(vec_count, -1))
        )
        mixed = 0.5 * (forward + lax.psum_scatter(spread, "rows", scatter_dimension=1, tiled=True))
        carried = mixed
    partial_gram = jnp.dot(carried, carried.T, precision=lax.Precision.HIGHEST)
    gram_matrix = lax.psum(partial_gram, "rows")
    cholesky_factor = jnp.linalg.cholesky(gram_matrix)
    carried = jax.scipy.linalg.solve_triangular(cholesky_factor, carried, lower=True)
    return (affinity, carried)


def solution(mesh):
    placed = (
        P(("groups", "rows"), None),
        P(("groups", "rows")),
        P(None, ("groups", "rows")),
        P(None, ("groups", "rows")),
        P(),
        P(),
    )
    return jax.shard_map(
        on_device,
        mesh=mesh,
        in_specs=placed,
        out_specs=(P(None, ("groups", "rows")), P(None, ("groups", "rows"))),
        check_vma=False,
    )
```

profile of v0, /device:TPU:0, one launch (start us, length us, event | category | flops | bytes accessed | tf_op | source)
XLA Modules:
  0.0 474.0 jit_solution(6266484893465082726)
XLA Ops:
  8.2 1.3 collective-permute-start
  11.5 2.9 multiply_reduce_fusion
  15.4 25.2 %all_gather.13 = f32[32,2048]{1,0:T(8,128)S(1)} all-gather(f32[32,128]{1,0:T(8,128)S(1)} %convert_multiply_fusion), channel_id=1, replica_groups=mesh['groups'=2,'rows'=16] {'rows'}, dimensions={1}, use_global_device_ids=true | all-gather | bytes 278528 | tf_op jit(solution)/shard_map/all_gather | solution.py:67
  41.1 14.1 %gather_fusion.1 = f32[4096,32]{1,0:T(8,128)} fusion(f32[32,2048]{0,1:T(8,128)S(1)} %copy.50, s32[4096]{0:T(1024)S(1)} %bitcast_clamp_fusion), kind=kCustom, calls=%fused_computation.clone | custom fusion | bytes 1064960 | tf_op jit(solution)/shard_map/jit(_take)/gather | solution.py:73
  55.2 3.1 all-gather.2.cloned.1.call-done
  58.3 1.7 fusion.64
  60.0 32.8 %gather_fusion = f32[4096]{0:T(1024)S(1)} fusion(f32[128,2048]{1,0:T(8,128)S(1)} %fusion.64, s32[4096]{0:T(1024)S(1)} %reshape.113), kind=kCustom, calls=%fused_computation.3 | custom fusion | bytes 65536 | tf_op jit(solution)/shard_map/while/body/eval_jaxpr/jit(take_along_axis)/gather | solution.py:56
  93.6 23.4 %scatter_custom_fusion = f32[32,2048]{0,1:T(8,128)} fusion(s32[4096]{0:T(1024)S(1)} %bitcast.98, f32[32,4096]{0,1:T(8,128)S(1)} %bitcast_multiply_fusion.4, f32[]{:T(128)} %constant.102.clone.1), kind=kCustom, calls=%fused_computation.22 | custom fusion | flops 131072 | bytes 2359300 | tf_op jit(solution)/shard_map/scatter-add | solution.py:77
  117.1 3.2 fusion.12
  120.3 53.4 %reduce-scatter.4.cloned.1.call-done = f32[32,128]{0,1:T(8,128)} async-done(((f32[32,2048]{0,1:T(8,128)}), f32[32,128]{0,1:T(8,128)}) %reduce-scatter.4.cloned.1.call-update) | async-done | bytes 16400 | tf_op jit(solution)/shard_map/reduce_scatter | solution.py:79
  174.6 22.6 %all_gather.14 = f32[32,2048]{0,1:T(8,128)S(1)} all-gather(f32[32,128]{0,1:T(8,128)S(1)} %add_multiply_fusion.2), channel_id=1, replica_groups=mesh['groups'=2,'rows'=16] {'rows'}, dimensions={1}, use_global_device_ids=true | all-gather | bytes 278528 | tf_op jit(solution)/shard_map/all_gather | solution.py:67
  197.1 1.8 fusion.65
  199.0 2.9 cholesky.59
  203.3 2.4 custom-call.13
  208.4 23.4 %scatter_custom_fusion.1 = f32[32,2048]{0,1:T(8,128)} fusion(s32[4096]{0:T(1024)S(1)} %bitcast.99, f32[32,4096]{0,1:T(8,128)S(1)} %bitcast_multiply_fusion.2, f32[]{:T(128)} %constant.102.clone.1), kind=kCustom, calls=%fused_computation.17 | custom fusion | flops 131072 | bytes 2359300 | tf_op jit(solution)/shard_map/scatter-add | solution.py:77
  232.0 1.3 copy.54
  233.3 14.1 %gather_fusion.2 = f32[4096,32]{1,0:T(8,128)} fusion(f32[32,2048]{0,1:T(8,128)S(1)} %copy.54, s32[4096]{0:T(1024)S(1)} %bitcast_clamp_fusion), kind=kCustom, calls=%fused_computation.1.clone | custom fusion | bytes 1064960 | tf_op jit(solution)/shard_map/jit(_take)/gather | solution.py:73
  247.4 3.2 fusion.9
  250.6 36.3 %reduce-scatter.6.cloned.1.call-done = f32[32,128]{0,1:T(8,128)} async-done(((f32[32,2048]{0,1:T(8,128)}), f32[32,128]{0,1:T(8,128)}) %reduce-scatter.6.cloned.1.call-update) | async-done | bytes 16400 | tf_op jit(solution)/shard_map/reduce_scatter | solution.py:79
  287.8 22.6 %all_gather.15 = f32[32,2048]{0,1:T(8,128)S(1)} all-gather(f32[32,128]{0,1:T(8,128)S(1)} %add_multiply_fusion.1), channel_id=1, replica_groups=mesh['groups'=2,'rows'=16] {'rows'}, dimensions={1}, use_global_device_ids=true | all-gather | bytes 278528 | tf_op jit(solution)/shard_map/all_gather | solution.py:67
  310.3 1.8 fusion.66
  312.2 2.9 cholesky.70
  316.5 2.4 custom-call.14
  321.6 23.4 %scatter_custom_fusion.2 = f32[32,2048]{0,1:T(8,128)} fusion(s32[4096]{0:T(1024)S(1)} %bitcast.100, f32[32,4096]{0,1:T(8,128)S(1)} %bitcast_multiply_fusion, f32[]{:T(128)} %constant.102.clone.1), kind=kCustom, calls=%fused_computation.12 | custom fusion | flops 131072 | bytes 2359300 | tf_op jit(solution)/shard_map/scatter-add | solution.py:77
  345.0 1.3 copy.57
  346.3 14.1 %gather_fusion.3 = f32[4096,32]{1,0:T(8,128)} fusion(f32[32,2048]{0,1:T(8,128)S(1)} %copy.57, s32[4096]{0:T(1024)S(1)} %bitcast_clamp_fusion), kind=kCustom, calls=%fused_computation.2.clone | custom fusion | bytes 1064960 | tf_op jit(solution)/shard_map/jit(_take)/gather | solution.py:73
  360.4 3.2 fusion.6
  363.6 36.6 %reduce-scatter.8.cloned.1.call-done = f32[32,128]{0,1:T(8,128)} async-done(((f32[32,2048]{0,1:T(8,128)}), f32[32,128]{0,1:T(8,128)}) %reduce-scatter.8.cloned.1.call-update) | async-done | bytes 16400 | tf_op jit(solution)/shard_map/reduce_scatter | solution.py:79
  401.3 57.6 %psum.7 = f32[32,32]{0,1:T(8,128)S(1)} all-reduce(f32[32,32]{0,1:T(8,128)S(1)} %fusion.39), channel_id=1, replica_groups=mesh['groups'=2,'rows'=16] {'rows'}, use_global_device_ids=true, to_apply=%region_12.16 | all-reduce | flops 1024 | bytes 8192 | tf_op jit(solution)/shard_map/psum | solution.py:82
  459.0 2.9 cholesky.81
  463.3 2.4 custom-call.9
  465.7 1.7 fusion.38
  (67 shorter events, 17.9 us)
Async XLA Ops:
  7.2 4.3 copy-start
  7.2 51.1 %all-gather.2.cloned.1.call-start = ((), (), s32[]{:S(2)}) async-start(), calls=%async_computation.3 | async-start | bytes 1114112 | tf_op jit(solution)/shard_map/all_gather | solution.py:44
  8.2 3.2 collective-permute-start
  11.5 3.7 copy-start.5
  11.5 3.9 copy-start.6
  15.1 158.6 %reduce-scatter.4.cloned.1.call-start = ((), (), s32[]{:S(2)}) async-start(), calls=%async_computation.4 | async-start | bytes 1114112 | tf_op jit(solution)/shard_map/reduce_scatter | solution.py:79
  41.0 17.3 %copy-start.4 = (bf16[128,256]{1,0:T(8,128)(2,1)S(1)}, bf16[128,256]{1,0:T(8,128)(2,1)}, u32[]{:S(2)}) copy-start(bf16[128,256]{1,0:T(8,128)(2,1)} %multiply_convert_fusion) | copy-start | bytes 196612
  93.0 267.4 %copy-start.3 = (f32[32,128]{1,0:T(8,128)}, f32[32,128]{1,0:T(8,128)S(1)}, u32[]{:S(2)}) copy-start(f32[32,128]{1,0:T(8,128)S(1)} %copy.61) | copy-start | bytes 49156
  117.0 169.9 %reduce-scatter.6.cloned.1.call-start = ((), (), s32[]{:S(2)}) async-start(), calls=%async_computation.5 | async-start | bytes 1114112 | tf_op jit(solution)/shard_map/reduce_scatter | solution.py:79
  206.9 0.7 copy-start.2
  231.8 168.4 %reduce-scatter.8.cloned.1.call-start = ((), (), s32[]{:S(2)}) async-start(), calls=%async_computation.6 | async-start | bytes 1114112 | tf_op jit(solution)/shard_map/reduce_scatter | solution.py:79
  320.2 0.7 copy-start.1
Sparse Core Ops, SparseCore 0:
  15.2 43.0 all-gather.1
  117.1 56.5 reduce-scatter.3
  231.9 54.9 reduce-scatter.5
  345.1 55.0 reduce-scatter.7
where the time goes:
time: 475 us; the launch traced here: 474 us
  waiting for transfers between devices  131 us (28%)
  blocking collectives  128 us (27%)
  other arithmetic  105 us (22%)
  local copies, waits for them, and re-layouts  81.2 us (17%)
  between operations  14 us (3%)
  matrix products  13.5 us (3%)
    reduce_scatter x3, waiting for transfers between devices, on_device(): lax.psum_scatter(spread, 'rows', scatter_dimension=1, tiled=True)  126 us
    all_gather x3, blocking collectives, on_device(): gathered = lax.all_gather(carried, 'rows', axis=1, tiled=True)  70.3 us
    scatter-add x3, other arithmetic, on_device(): spread = jnp.zeros((vec_count, gathered.shape[1]), jnp.float32).at[:, nei...  70.2 us
    psum x1, blocking collectives, on_device(): gram_matrix = lax.psum(partial_gram, 'rows')  57.6 us
    gather x3, local copies, waits for them, and re-layouts, on_device(): jnp.take(gathered, neighbours, axis=1)  42.3 us
    gather x3, local copies, waits for them, and re-layouts, one_block(): jnp.take_along_axis(scores, jnp.clip(relative, 0, block_cols - 1).T, axis=1)  32.9 us
    another operation x9, other arithmetic, on_device(): cholesky_factor = jnp.linalg.cholesky(gram_matrix)  10.8 us
    reduce_sum x3, other arithmetic, on_device(): jnp.sum(affinity[None] * jnp.take(gathered, neighbours, axis=1), axis=1)  9.57 us
  transfers between devices with their start and end apart: 5, of which 5 were waited for; matrix products, arithmetic and copies ran while one was open for 12% of the time, Pallas kernels for 0%

commit v1 on v0

--- a/solution.py
+++ b/solution.py
@@ -64,7 +64,7 @@
     vec_count = vectors.shape[0]
     carried = vectors
     for turn_index in range(ITERS):
-        gathered = lax.all_gather(carried, "rows", axis=1, tiled=True)
+        gathered = jnp.concatenate(lax.all_gather(carried, "rows"), axis=1)
         if turn_index > 0:
             gram_matrix = jnp.dot(gathered, gathered.T, precision=lax.Precision.HIGHEST)
             cholesky_factor = jnp.linalg.cholesky(gram_matrix)

time: 475 us -> 466 us (0.981)
  local copies, waits for them, and re-layouts: 81.2 us -> 88 us
  waiting for transfers between devices: 131 us -> 125 us
  blocking collectives: 128 us -> 123 us
  matrix products: 13.5 us -> 8.63 us
    scatter-add x0 -> x3, local copies, waits for them, and re-layouts: none -> 6.77 us  [on_device(): spread = jnp.zeros((vec_count, gathered.shape[1]), jnp.float32).at[:, nei...]
    reduce_scatter x3, waiting for transfers between devices: 126 us -> 121 us  [on_device(): lax.psum_scatter(spread, 'rows', scatter_dimension=1, tiled=True)]
where the time goes in v1:
time: 466 us; the launch traced here: 465 us
  waiting for transfers between devices  125 us (27%)
  blocking collectives  123 us (26%)
  other arithmetic  105 us (23%)
  local copies, waits for them, and re-layouts  88 us (19%)
  between operations  14 us (3%)
  matrix products  8.63 us (2%)
    reduce_scatter x3, waiting for transfers between devices, on_device(): lax.psum_scatter(spread, 'rows', scatter_dimension=1, tiled=True)  121 us
    scatter-add x3, other arithmetic, on_device(): spread = jnp.zeros((vec_count, gathered.shape[1]), jnp.float32).at[:, nei...  70.2 us
    all_gather x3, blocking collectives, on_device(): gathered = jnp.concatenate(lax.all_gather(carried, 'rows'), axis=1)  65.7 us
    psum x1, blocking collectives, on_device(): gram_matrix = lax.psum(partial_gram, 'rows')  57.6 us
    gather x3, local copies, waits for them, and re-layouts, on_device(): jnp.take(gathered, neighbours, axis=1)  42.3 us
    gather x3, local copies, waits for them, and re-layouts, one_block(): jnp.take_along_axis(scores, jnp.clip(relative, 0, block_cols - 1).T, axis=1)  32.9 us
    another operation x9, other arithmetic, on_device(): cholesky_factor = jnp.linalg.cholesky(gram_matrix)  10.8 us
    reduce_sum x3, other arithmetic, on_device(): jnp.sum(affinity[None] * jnp.take(gathered, neighbours, axis=1), axis=1)  9.57 us
  transfers between devices with their start and end apart: 5, of which 5 were waited for; matrix products, arithmetic and copies ran while one was open for 12% of the time, Pallas kernels for 0%

profile of v1, /device:TPU:0, one launch (start us, length us, event | category | flops | bytes accessed | tf_op | source)
XLA Modules:
  0.0 465.1 jit_solution(18267725946760163365)
XLA Ops:
  8.2 1.3 collective-permute-start
  11.5 2.9 multiply_reduce_fusion
  15.4 25.2 %all-gather = f32[512,128]{1,0:T(8,128)S(1)} all-gather(f32[32,128]{1,0:T(8,128)S(1)} %convert_multiply_fusion), channel_id=2, replica_groups=mesh['groups'=2,'rows'=16] {'rows'}, dimensions={0}, use_global_device_ids=true | all-gather | bytes 278528 | tf_op jit(solution)/shard_map/all_gather | solution.py:67
  40.9 14.1 %gather_fusion.1 = f32[4096,32]{1,0:T(8,128)} fusion(f32[32,2048]{0,1:T(8,128)S(1)} %bitcast.111, s32[4096]{0:T(1024)S(1)} %bitcast_clamp_fusion), kind=kCustom, calls=%fused_computation.clone | custom fusion | bytes 1064960 | tf_op jit(solution)/shard_map/jit(_take)/gather | solution.py:73
  55.1 3.2 all-gather.5.cloned.1.call-done
  58.3 1.7 fusion.68
  60.0 32.8 %gather_fusion = f32[4096]{0:T(1024)S(1)} fusion(f32[128,2048]{1,0:T(8,128)S(1)} %fusion.68, s32[4096]{0:T(1024)S(1)} %reshape.137), kind=kCustom, calls=%fused_computation.3 | custom fusion | bytes 65536 | tf_op jit(solution)/shard_map/while/body/eval_jaxpr/jit(take_along_axis)/gather | solution.py:56
  93.6 23.4 %scatter_custom_fusion = f32[32,2048]{0,1:T(8,128)} fusion(s32[4096]{0:T(1024)S(1)} %bitcast.125, f32[32,4096]{0,1:T(8,128)S(1)} %bitcast_multiply_fusion.4, f32[]{:T(128)} %constant.102.clone.1), kind=kCustom, calls=%fused_computation.22 | custom fusion | flops 131072 | bytes 2359300 | tf_op jit(solution)/shard_map/scatter-add | solution.py:77
  117.0 2.3 copy.101
  119.3 3.2 fusion.12
  122.6 51.5 %reduce-scatter.4.cloned.1.call-done = f32[32,128]{1,0:T(8,128)} async-done(((f32[32,2048]{1,0:T(8,128)}), f32[32,128]{1,0:T(8,128)}) %reduce-scatter.4.cloned.1.call-update) | async-done | bytes 16400 | tf_op jit(solution)/shard_map/reduce_scatter | solution.py:79
  174.9 20.1 %all-gather.1 = f32[512,128]{1,0:T(8,128)S(1)} all-gather(f32[32,128]{1,0:T(8,128)S(1)} %add_multiply_fusion.2), channel_id=3, replica_groups=mesh['groups'=2,'rows'=16] {'rows'}, dimensions={0}, use_global_device_ids=true | all-gather | bytes 278528 | tf_op jit(solution)/shard_map/all_gather | solution.py:67
  195.4 2.9 cholesky.59
  199.7 2.4 custom-call.13
  204.0 23.4 %scatter_custom_fusion.1 = f32[32,2048]{0,1:T(8,128)} fusion(s32[4096]{0:T(1024)S(1)} %bitcast.126, f32[32,4096]{0,1:T(8,128)S(1)} %bitcast_multiply_fusion.2, f32[]{:T(128)} %constant.102.clone.1), kind=kCustom, calls=%fused_computation.17 | custom fusion | flops 131072 | bytes 2359300 | tf_op jit(solution)/shard_map/scatter-add | solution.py:77
  227.4 2.3 copy.107
  229.8 1.3 copy.105
  231.0 14.1 %gather_fusion.2 = f32[4096,32]{1,0:T(8,128)} fusion(f32[32,2048]{0,1:T(8,128)S(1)} %copy.105, s32[4096]{0:T(1024)S(1)} %bitcast_clamp_fusion), kind=kCustom, calls=%fused_computation.1.clone | custom fusion | bytes 1064960 | tf_op jit(solution)/shard_map/jit(_take)/gather | solution.py:73
  245.1 3.2 fusion.9
  248.4 34.5 %reduce-scatter.6.cloned.1.call-done = f32[32,128]{1,0:T(8,128)} async-done(((f32[32,2048]{1,0:T(8,128)}), f32[32,128]{1,0:T(8,128)}) %reduce-scatter.6.cloned.1.call-update) | async-done | bytes 16400 | tf_op jit(solution)/shard_map/reduce_scatter | solution.py:79
  283.6 20.3 %all-gather.2 = f32[512,128]{1,0:T(8,128)S(1)} all-gather(f32[32,128]{1,0:T(8,128)S(1)} %add_multiply_fusion.1), channel_id=4, replica_groups=mesh['groups'=2,'rows'=16] {'rows'}, dimensions={0}, use_global_device_ids=true | all-gather | bytes 278528 | tf_op jit(solution)/shard_map/all_gather | solution.py:67
  304.3 2.9 cholesky.70
  308.6 2.4 custom-call.14
  312.9 23.4 %scatter_custom_fusion.2 = f32[32,2048]{0,1:T(8,128)} fusion(s32[4096]{0:T(1024)S(1)} %bitcast.127, f32[32,4096]{0,1:T(8,128)S(1)} %bitcast_multiply_fusion, f32[]{:T(128)} %constant.102.clone.1), kind=kCustom, calls=%fused_computation.12 | custom fusion | flops 131072 | bytes 2359300 | tf_op jit(solution)/shard_map/scatter-add | solution.py:77
  336.3 2.3 copy.113
  339.9 14.1 %gather_fusion.3 = f32[4096,32]{1,0:T(8,128)} fusion(f32[32,2048]{0,1:T(8,128)S(1)} %copy.111, s32[4096]{0:T(1024)S(1)} %bitcast_clamp_fusion), kind=kCustom, calls=%fused_computation.2.clone | custom fusion | bytes 1064960 | tf_op jit(solution)/shard_map/jit(_take)/gather | solution.py:73
  353.9 3.2 fusion.6
  357.2 34.5 %reduce-scatter.8.cloned.1.call-done = f32[32,128]{1,0:T(8,128)} async-done(((f32[32,2048]{1,0:T(8,128)}), f32[32,128]{1,0:T(8,128)}) %reduce-scatter.8.cloned.1.call-update) | async-done | bytes 16400 | tf_op jit(solution)/shard_map/reduce_scatter | solution.py:79
  392.7 57.6 %psum.7 = f32[32,32]{0,1:T(8,128)S(1)} all-reduce(f32[32,32]{0,1:T(8,128)S(1)} %fusion.58), channel_id=1, replica_groups=mesh['groups'=2,'rows'=16] {'rows'}, use_global_device_ids=true, to_apply=%region_12.16 | all-reduce | flops 1024 | bytes 8192 | tf_op jit(solution)/shard_map/psum | solution.py:82
  450.3 2.9 cholesky.81
  454.6 2.4 custom-call.9
  457.0 1.6 fusion.47
  (72 shorter events, 17.8 us)
Async XLA Ops:
  7.2 4.3 copy-start
  7.2 51.1 %all-gather.5.cloned.1.call-start = ((), (), s32[]{:S(2)}) async-start(), calls=%async_computation.3 | async-start | bytes 1114112 | tf_op jit(solution)/shard_map/all_gather | solution.py:44
  8.2 3.2 collective-permute-start
  11.5 3.7 copy-start.5
  11.5 3.9 copy-start.6
  15.1 159.1 %reduce-scatter.4.cloned.1.call-start = ((), (), s32[]{:S(2)}) async-start(), calls=%async_computation.4 | async-start | bytes 278528 | tf_op jit(solution)/shard_map/reduce_scatter | solution.py:79
  40.9 17.4 %copy-start.4 = (bf16[128,256]{1,0:T(8,128)(2,1)S(1)}, bf16[128,256]{1,0:T(8,128)(2,1)}, u32[]{:S(2)}) copy-start(bf16[128,256]{1,0:T(8,128)(2,1)} %multiply_convert_fusion) | copy-start | bytes 196612
  93.0 261.0 %copy-start.3 = (f32[32,128]{1,0:T(8,128)}, f32[32,128]{1,0:T(8,128)S(1)}, u32[]{:S(2)}) copy-start(f32[32,128]{1,0:T(8,128)S(1)} %copy.117) | copy-start | bytes 49156
  119.3 163.6 %reduce-scatter.6.cloned.1.call-start = ((), (), s32[]{:S(2)}) async-start(), calls=%async_computation.5 | async-start | bytes 278528 | tf_op jit(solution)/shard_map/reduce_scatter | solution.py:79
  202.6 0.7 copy-start.2
  229.7 162.0 %reduce-scatter.8.cloned.1.call-start = ((), (), s32[]{:S(2)}) async-start(), calls=%async_computation.6 | async-start | bytes 278528 | tf_op jit(solution)/shard_map/reduce_scatter | solution.py:79
  311.5 0.7 copy-start.1
Sparse Core Ops, SparseCore 0:
  15.2 43.0 all-gather.4
  119.4 54.6 reduce-scatter.3
  229.8 52.9 reduce-scatter.5
  338.7 52.9 reduce-scatter.7
